TPU v7x, 32 devices: a whole 2x2x4 slice. The times are simulated.
32 devices in a mesh: fsdp: 4 (over x, core), tm: 8 (over z, y).
Axes of the slice: x: 2, y: 2, z: 4, core: 2. Of those that a mesh axis runs over, the one named last changes fastest.
Arguments:
- tokens: bfloat16 [8, 8, 256, 1024], P('fsdp', 'tm'), may hold values from -6 to 6
- spatial_gain: float32 [1024], replicated, may hold values from 0.25 to 1.75
- spatial_qkv: bfloat16 [1024, 1536], P('fsdp'), may hold values from -16 to 16
- spatial_out: bfloat16 [512, 1024], P('fsdp'), may hold values from -0.25 to 0.25
- temporal_gain: float32 [1024], replicated, may hold values from 0.25 to 1.75
- temporal_qkv: bfloat16 [1024, 1536], P('fsdp'), may hold values from -16 to 16
- temporal_out: bfloat16 [512, 1024], P('fsdp'), may hold values from -0.25 to 0.25
Outputs:
- encoded: bfloat16 [8, 8, 256, 1024], P('fsdp', 'tm')
All inputs are finite; a program needn't handle non-finite values.
Results may differ from a plain program's by a relative error of at most 0.0061.
Values may be sent and summed in bfloat16 or wider, within the bound.
A program may use at most 64 MiB of HBM per device.

v0:
```python
import jax
import jax.numpy as jnp
from jax import lax
from jax.sharding import PartitionSpec as P

HEAD = 64
HEADS = 8
INNER = 512
EPSILON = 1e-06


def norm_rows(source, norm_gain):
    values = source.astype(jnp.float32)
    centre = values - jnp.mean(values, axis=-1, keepdims=True)
    spread = jnp.mean(centre * centre, axis=-1, keepdims=True)
    return (centre * lax.rsqrt(spread + EPSILON) * norm_gain).astype(jnp.bfloat16)


def attention_core(projected):
    inner_width = projected.shape[-1] // 3
    lead_shape = projected.shape[:-1]
    queries = projected[..., :inner_width].reshape(lead_shape + (HEADS, HEAD))
    key_rows = projected[..., inner_width : 2 * inner_width].reshape(lead_shape + (HEADS, HEAD))
    value_rows = (
        projected[..., 2 * inner_width :].astype(jnp.bfloat16).reshape(lead_shape + (HEADS, HEAD))
    )
    scores = jnp.einsum(
        "blmhe,bkmhe->bmhlk", queries, key_rows, precision=lax.Precision.HIGHEST
    ) * HEAD ** (-0.5)
    row_max = jnp.max(scores, axis=-1, keepdims=True)
    exponent = jnp.exp(scores - row_max)
    weights = (exponent / jnp.sum(exponent, axis=-1, keepdims=True)).astype(jnp.bfloat16)
    context = jnp.einsum(
        "bmhlk,bkmhe->blmhe", weights, value_rows, preferred_element_type=jnp.float32
    )
    return context.astype(jnp.bfloat16).reshape(lead_shape + (inner_width,))


def project_inputs(normed, weight):

    def add_rows(running, segment, offset):
        return jnp.dot(normed, segment, preferred_element_type=jnp.float32)

    initial = jnp.zeros((normed.shape[0], weight.shape[1]), jnp.float32)
    return add_rows(initial, lax.all_gather(weight, "fsdp", axis=0, tiled=True), jnp.int32(0))


def project_outputs(context, weight):

    def add_rows(running, segment, offset):
        return jnp.dot(context, segment, preferred_element_type=jnp.float32)

    initial = jnp.zeros((context.shape[0], weight.shape[1]), jnp.float32)
    return add_rows(initial, lax.all_gather(weight, "fsdp", axis=0, tiled=True), jnp.int32(0))


def shards(
    tokens, spatial_gain, spatial_qkv, spatial_out, temporal_gain, temporal_qkv, temporal_out
):
    clip_count, frames, places, feature_width = tokens.shape
    row_count = clip_count * frames * places
    normed = norm_rows(tokens, spatial_gain).reshape(row_count, feature_width)
    projected = project_inputs(normed, spatial_qkv).reshape(
        clip_count * frames, places, 1, 3 * INNER
    )
    context = attention_core(projected).reshape(row_count, INNER)
    middle = (
        tokens.reshape(row_count, feature_width).astype(jnp.float32)
        + project_outputs(context, spatial_out)
    ).astype(jnp.bfloat16)
    middle = middle.reshape(clip_count, frames, places, feature_width)
    arrived = lax.all_to_all(middle, "tm", split_axis=2, concat_axis=1, tiled=True)
    full_frames = arrived.shape[1]
    few_places = arrived.shape[2]
    normed_t = norm_rows(arrived, temporal_gain).reshape(row_count, feature_width)
    projected_t = project_inputs(normed_t, temporal_qkv).reshape(
        clip_count, full_frames, few_places, 3 * INNER
    )
    context_t = attention_core(projected_t)
    returned_ctx = lax.all_to_all(context_t, "tm", split_axis=1, concat_axis=2, tiled=True)
    finished = middle.reshape(row_count, feature_width).astype(jnp.float32) + project_outputs(
        returned_ctx.reshape(row_count, INNER), temporal_out
    )
    return finished.astype(jnp.bfloat16).reshape(clip_count, frames, places, feature_width)


def solution(mesh):
    placed = (
        P("fsdp", "tm", None, None),
        P(),
        P("fsdp", None),
        P("fsdp", None),
        P(),
        P("fsdp", None),
        P("fsdp", None),
    )
    return jax.shard_map(
        shards, mesh=mesh, in_specs=placed, out_specs=P("fsdp", "tm", None, None), check_vma=False
    )
```

profile of v0, /device:TPU:0, one launch (start us, length us, event | category | flops | bytes accessed | tf_op | source)
XLA Modules:
  0.0 167.2 jit_solution(3869164747820133010)
XLA Ops:
  6.5 0.7 all-gather.5.cloned.1.call-update
  7.3 0.7 all-gather.7.cloned.1.call-update
  8.1 0.7 all-gather.9.cloned.1.call-update
  9.4 30.8 %all-gather.5.cloned.1.call-done = bf16[1024,1536]{1,0:T(8,128)(2,1)} async-done(((bf16[256,1536]{1,0:T(8,128)(2,1)}), bf16[1024,1536]{1,0:T(8,128)(2,1)}) %all-gather.5.cloned.1.call-update) | async-done | bytes 3145744 | tf_op jit(solution)/shard_map/all_gather | solution.py:45
  40.2 3.8 %convolution_bitcast_fusion = f32[2,256,1,1536]{3,1,0,2:T(8,128)S(1)} fusion(bf16[1024,1536]{1,0:T(8,128)(2,1)} %all-gather.5.cloned.1.call-done, bf16[2,1,256,1024]{3,2,1,0:T(8,128)(2,1)S(1)} %copy-done, f32[1024]{0:T(1024)S(1)} %copy-done.5, f32[2,256]{1,0:T(2,128)S(1)} %add_rsqrt_fusion.1, f32[2,256]{1,0:T(2,128)S(1)} %broadcast_multiply_fusion.1), kind=kOutput, calls=%fused_computation.6 | convolution fusion | flops 1613234176 | bytes 7348224 | tf_op jit(solution)/shard_map/dot_general | solution.py:42
  44.0 1.7 %copy-done.1 = f32[2,256,1,1536]{3,1,0,2:T(8,128)} copy-done((f32[2,256,1,1536]{3,1,0,2:T(8,128)}, f32[2,256,1,1536]{3,1,0,2:T(8,128)S(1)}, u32[]{:S(2)}) %copy-start.1) | copy-done | bytes 3145752
  45.7 1.0 copy.81
  46.7 2.8 %fusion.36 = (f32[2,256,1,512]{3,1,0,2:T(8,128)S(1)}, f32[2,256,1,512]{3,1,0,2:T(8,128)}) fusion(f32[2,256,1,1536]{3,1,0,2:T(8,128)} %copy-done.1), kind=kLoop, calls=%fused_computation.54 | loop fusion | bytes 4194304 | tf_op jit(solution)/shard_map/slice | solution.py:23
  49.5 1.6 copy.82
  51.1 1.3 copy.83
  52.4 4.7 %fusion.39 = f32[2,8,256,256]{2,3,1,0:T(8,128)S(1)} fusion(f32[2,256,8,64]{1,3,2,0:T(8,128)S(1)} %bitcast.58, f32[2,256,8,64]{1,3,2,0:T(8,128)} %bitcast.59), kind=kOutput, calls=%fused_computation.57 | convolution fusion | flops 805306368 | bytes 6291456 | tf_op jit(solution)/shard_map/blmhe,bkmhe->bmhlk/dot_general | solution.py:27
  57.2 3.2 %fusion.37 = (f32[2,8,256]{2,1,0:T(8,128)S(1)}, f32[2,8,256,256]{2,3,1,0:T(8,128)S(1)}) fusion(f32[2,8,256,256]{2,3,1,0:T(8,128)S(1)} %fusion.39), kind=kOutput, calls=%fused_computation.55 | output fusion | flops 4194559 | bytes 8404992 | tf_op jit(solution)/shard_map/sub | solution.py:31
  61.6 2.0 %fusion.8 = bf16[512,1024]{1,0:T(8,128)(2,1)S(1)} fusion(bf16[2,1,256,1024]{3,2,1,0:T(8,128)(2,1)S(1)} %copy-done, bf16[512,512]{0,1:T(8,128)(2,1)S(1)} %bitcast.65, bf16[512,1024]{1,0:T(8,128)(2,1)} %all-gather.7.cloned.1.call-done), kind=kOutput, calls=%fused_computation.11 | convolution fusion | flops 538443776 | bytes 3670016 | tf_op jit(solution)/shard_map/dot_general | solution.py:51
  63.6 1.0 copy-done.2
  64.5 2.0 %copy.86 = bf16[2,1,256,1024]{3,0,1,2:T(2,128)(2,1)} copy(bf16[2,1,256,1024]{3,2,0,1:T(8,128)(2,1)S(1)} %bitcast.62) | data formatting | bytes 2097152 | tf_op jit(solution)/shard_map/reshape | solution.py:71
  66.6 5.5 %all-to-all-start = ((bf16[2,1,256,1024]{3,0,1,2:T(2,128)(2,1)}), bf16[2,1,256,1024]{3,0,1,2:T(2,128)(2,1)S(1)}, u32[]{:S(2)}, u32[]{:S(2)}) async-start(bf16[2,1,256,1024]{3,0,1,2:T(2,128)(2,1)} %copy.86), calls=%async_computation | async-start | bytes 2097152 | tf_op jit(solution)/shard_map/all_to_all | solution.py:72
  72.6 25.6 %all-to-all-done = bf16[2,1,256,1024]{3,0,1,2:T(2,128)(2,1)S(1)} async-done(((bf16[2,1,256,1024]{3,0,1,2:T(2,128)(2,1)}), bf16[2,1,256,1024]{3,0,1,2:T(2,128)(2,1)S(1)}, u32[]{:S(2)}, u32[]{:S(2)}) %all-to-all-start) | async-done | bytes 1048608 | tf_op jit(solution)/shard_map/all_to_all | solution.py:72
  98.3 0.7 convert.12
  99.0 0.9 convert_reduce_fusion.1
  99.9 2.0 %multiply_reduce_fusion.1 = f32[2,256]{0,1:T(8,128)S(1)} fusion(bf16[2,1,256,1024]{3,0,1,2:T(2,128)(2,1)S(1)} %all-to-all-done, f32[2,256]{0,1:T(8,128)S(1)} %broadcast_multiply_fusion), kind=kLoop, calls=%fused_computation.22 | loop fusion | flops 2096640 | bytes 1052672 | tf_op jit(solution)/shard_map/reduce_sum | solution.py:15
  102.2 4.0 %fusion.5 = f32[2,8,32,1536]{3,2,1,0:T(8,128)S(1)} fusion(bf16[1024,1536]{1,0:T(8,128)(2,1)} %all-gather.9.cloned.1.call-done, f32[2,8,32,1024]{3,0,2,1:T(2,128)S(1)} %convert.12, f32[1024]{0:T(1024)S(1)} %copy-done.6, f32[2,8,32]{2,1,0:T(8,128)S(1)} %copy.121, f32[2,8,32]{2,1,0:T(8,128)S(1)} %copy.122), kind=kOutput, calls=%fused_computation.7 | convolution fusion | flops 1612709888 | bytes 8396800 | tf_op jit(solution)/shard_map/dot_general | solution.py:42
  106.2 1.1 fusion.35
  107.4 0.9 slice.34
  108.2 1.6 reshape.157
  109.8 1.8 %reshape.156 = f32[2,8,32,8,64]{4,3,2,1,0:T(8,128)} reshape(f32[2,8,32,512]{3,2,1,0:T(8,128)S(1)} %get-tuple-element.5) | data formatting | bytes 2097152 | tf_op jit(solution)/shard_map/reshape | solution.py:22
  111.6 1.6 reshape.155
  113.2 7.9 %fusion.9 = f32[2,32,8,8,8]{3,4,2,1,0:T(8,128)S(1)} fusion(f32[2,8,32,8,64]{4,3,2,1,0:T(8,128)S(1)} %reshape.157, f32[2,8,32,8,64]{4,3,2,1,0:T(8,128)} %reshape.156), kind=kOutput, calls=%fused_computation.12 | convolution fusion | flops 25165824 | bytes 2228224 | tf_op jit(solution)/shard_map/blmhe,bkmhe->bmhlk/dot_general | solution.py:27
  121.1 16.6 %fusion.38 = (f32[2,32,8,8]{3,2,1,0:T(8,128)S(1)}, f32[2,32,8,8,8]{3,4,2,1,0:T(8,128)S(1)}) fusion(f32[2,32,8,8,8]{3,4,2,1,0:T(8,128)S(1)} %fusion.9), kind=kOutput, calls=%fused_computation.56 | output fusion | flops 98311 | bytes 278528 | tf_op jit(solution)/shard_map/sub | solution.py:31
  137.7 1.0 fusion.18
  138.9 0.6 reshape.165
  139.6 18.1 %all_to_all.8 = bf16[2,8,32,512]{3,2,0,1:T(8,128)(2,1)S(1)} all-to-all(bf16[2,8,32,512]{3,2,0,1:T(8,128)(2,1)S(1)} %reshape.165), channel_id=1, replica_groups=mesh['fsdp'=4,'tm'=8] {'tm'}, dimensions={1} | all-to-all | bytes 1048576 | tf_op jit(solution)/shard_map/all_to_all | solution.py:80
  157.7 2.9 %add_convert_fusion = bf16[512,1024]{1,0:T(8,128)(2,1)} fusion(bf16[512,1024]{1,0:T(8,128)(2,1)S(1)} %copy-done.3, bf16[512,512]{1,0:T(8,128)(2,1)S(1)} %bitcast.64, bf16[512,1024]{1,0:T(8,128)(2,1)} %all-gather.11.cloned.1.call-done), kind=kOutput, calls=%fused_computation.19 | convolution fusion | flops 538443776 | bytes 3670016 | tf_op jit(solution)/shard_map/dot_general | solution.py:51
  (34 shorter events, 3.0 us)
Async XLA Ops:
  6.5 2.2 %copy-start = (bf16[2,1,256,1024]{3,2,1,0:T(8,128)(2,1)S(1)}, bf16[2,1,256,1024]{3,2,1,0:T(8,128)(2,1)}, u32[]{:S(2)}) copy-start(bf16[2,1,256,1024]{3,2,1,0:T(8,128)(2,1)} %param.7) | copy-start | bytes 3145732
  6.5 33.6 %copy-start.5 = (f32[1024]{0:T(1024)S(1)}, f32[1024]{0:T(1024)}, u32[]{:S(2)}) copy-start(f32[1024]{0:T(1024)} %param.8) | copy-start | bytes 12292
  6.5 33.6 %all-gather.5.cloned.1.call-start = ((), (), s32[]{:S(2)}) async-start(), calls=%async_computation.2 | async-start | bytes 3932160 | tf_op jit(solution)/shard_map/all_gather | solution.py:45
  7.3 54.3 %all-gather.7.cloned.1.call-start = ((), (), s32[]{:S(2)}) async-start(), calls=%async_computation.3 | async-start | bytes 1310720 | tf_op jit(solution)/shard_map/all_gather | solution.py:54
  8.0 94.2 %all-gather.9.cloned.1.call-start = ((), (), s32[]{:S(2)}) async-start(), calls=%async_computation.4 | async-start | bytes 3932160 | tf_op jit(solution)/shard_map/all_gather | solution.py:45
  44.0 1.7 %copy-start.1 = (f32[2,256,1,1536]{3,1,0,2:T(8,128)}, f32[2,256,1,1536]{3,1,0,2:T(8,128)S(1)}, u32[]{:S(2)}) copy-start(f32[2,256,1,1536]{3,1,0,2:T(8,128)S(1)} %convolution_bitcast_fusion) | copy-start | bytes 9437188
  57.2 3.3 %copy-start.4 = (bf16[2,256,1,512]{1,3,0,2:T(8,128)(2,1)S(1)}, bf16[2,256,1,512]{1,3,0,2:T(8,128)(2,1)}, u32[]{:S(2)}) copy-start(bf16[2,256,1,512]{1,3,0,2:T(8,128)(2,1)} %copy.81) | copy-start | bytes 1572868
  63.6 1.0 copy-start.2
  66.6 31.7 %all-to-all-start = ((bf16[2,1,256,1024]{3,0,1,2:T(2,128)(2,1)}), bf16[2,1,256,1024]{3,0,1,2:T(2,128)(2,1)S(1)}, u32[]{:S(2)}, u32[]{:S(2)}) async-start(bf16[2,1,256,1024]{3,0,1,2:T(2,128)(2,1)} %copy.86), calls=%async_computation | async-start | bytes 2097152 | tf_op jit(solution)/shard_map/all_to_all | solution.py:72
  72.1 85.6 %all-gather.11.cloned.1.call-start = ((), (), s32[]{:S(2)}) async-start(), calls=%async_computation.5 | async-start | bytes 1310720 | tf_op jit(solution)/shard_map/all_gather | solution.py:54
  99.0 3.2 %copy-start.6 = (f32[1024]{0:T(1024)S(1)}, f32[1024]{0:T(1024)}, u32[]{:S(2)}) copy-start(f32[1024]{0:T(1024)} %param.11) | copy-start | bytes 12292
  138.9 18.8 %copy-start.3 = (bf16[512,1024]{1,0:T(8,128)(2,1)S(1)}, bf16[512,1024]{1,0:T(8,128)(2,1)}, u32[]{:S(2)}) copy-start(bf16[512,1024]{1,0:T(8,128)(2,1)} %copy-done.2) | copy-start | bytes 3145732
Sparse Core Ops, SparseCore 0:
  8.9 31.2 all-gather.4
  41.7 16.6 all-gather.6
  60.0 28.4 all-gather.8
  90.0 16.6 all-gather.10
where the time goes:
time: 168 us; the launch traced here: 167 us
  waiting for transfers between devices  59 us (35%)
  matrix products  26.8 us (16%)
  other arithmetic  24.1 us (14%)
  local copies, waits for them, and re-layouts  20.1 us (12%)
  blocking collectives  18.1 us (11%)
  between operations  13.4 us (8%)
  starting transfers between devices  5.61 us (3%)
    all_gather x2, waiting for transfers between devices, project_inputs(): lax.all_gather(weight, 'fsdp', axis=0, tiled=True)  30.8 us
    all_to_all x1, waiting for transfers between devices, shards(): lax.all_to_all(middle, 'tm', split_axis=2, concat_axis=1, tiled=True)  25.6 us
    sub x2, other arithmetic, attention_core(): exponent = jnp.exp(scores - row_max)  19.8 us
    all_to_all x1, blocking collectives, shards(): lax.all_to_all(context_t, 'tm', split_axis=1, concat_axis=2, tiled=True)  18.1 us
    dot_general x2, matrix products, attention_core(): jnp.einsum('blmhe,bkmhe->bmhlk', queries, key_rows, precision=lax.Precisi...  12.6 us
    dot_general x2, matrix products, add_rows(): return jnp.dot(normed, segment, preferred_element_type=jnp.float32)  7.81 us
    all_to_all x1, starting transfers between devices, shards(): lax.all_to_all(middle, 'tm', split_axis=2, concat_axis=1, tiled=True)  5.5 us
    dot_general x2, matrix products, add_rows(): return jnp.dot(context, segment, preferred_element_type=jnp.float32)  4.86 us
  transfers between devices with their start and end apart: 5, of which 2 were waited for; matrix products, arithmetic and copies ran while one was open for 39% of the time, Pallas kernels for 0%

commit v1 on v0

--- a/solution.py
+++ b/solution.py
@@ -77,7 +77,11 @@
         clip_count, full_frames, few_places, 3 * INNER
     )
     context_t = attention_core(projected_t)
-    returned_ctx = lax.all_to_all(context_t, "tm", split_axis=1, concat_axis=2, tiled=True)
+    u_next = lax.axis_size("tm")
+    upper = jnp.stack(jnp.split(context_t, u_next, axis=1), axis=0)
+    returned_ctx = jnp.concatenate(
+        lax.all_to_all(upper, axis_name="tm", split_axis=0, concat_axis=0), axis=2
+    )
     finished = middle.reshape(row_count, feature_width).astype(jnp.float32) + project_outputs(
         returned_ctx.reshape(row_count, INNER), temporal_out
     )

time: 168 us -> 154 us (0.917)
  other arithmetic: 24.1 us -> 9.64 us
    sub x2, other arithmetic: 19.8 us -> 5.53 us  [attention_core(): exponent = jnp.exp(scores - row_max)]
  transfers between devices with their start and end apart: 5 -> 5, of which waited for: 2 -> 2; matrix products, arithmetic and copies ran while one was open for 39% -> 34% of each run, Pallas kernels for 0% -> 0%
where the time goes in v1:
time: 154 us; the launch traced here: 153 us
  waiting for transfers between devices  58.8 us (38%)
  matrix products  28.3 us (18%)
  local copies, waits for them, and re-layouts  19.1 us (12%)
  blocking collectives  18.1 us (12%)
  between operations  13.4 us (9%)
  other arithmetic  9.64 us (6%)
  starting transfers between devices  5.79 us (4%)
    all_gather x2, waiting for transfers between devices, project_inputs(): lax.all_gather(weight, 'fsdp', axis=0, tiled=True)  30.8 us
    all_to_all x1, waiting for transfers between devices, shards(): lax.all_to_all(middle, 'tm', split_axis=2, concat_axis=1, tiled=True)  25.6 us
    all_to_all x1, blocking collectives, shards(): lax.all_to_all(upper, axis_name='tm', split_axis=0, concat_axis=0)  18.1 us
    dot_general x2, matrix products, attention_core(): jnp.einsum('blmhe,bkmhe->bmhlk', queries, key_rows, precision=lax.Precisi...  12.6 us
    dot_general x2, matrix products, add_rows(): return jnp.dot(normed, segment, preferred_element_type=jnp.float32)  7.8 us
    sub x2, other arithmetic, attention_core(): exponent = jnp.exp(scores - row_max)  5.53 us
    all_to_all x1, starting transfers between devices, shards(): lax.all_to_all(middle, 'tm', split_axis=2, concat_axis=1, tiled=True)  5.49 us
    dot_general x2, matrix products, add_rows(): return jnp.dot(context, segment, preferred_element_type=jnp.float32)  4.86 us
  transfers between devices with their start and end apart: 5, of which 2 were waited for; matrix products, arithmetic and copies ran while one was open for 34% of the time, Pallas kernels for 0%

profile of v1, /device:TPU:0, one launch (start us, length us, event | category | flops | bytes accessed | tf_op | source)
XLA Modules:
  0.0 153.2 jit_solution(6390045680826206325)
XLA Ops:
  6.5 0.7 all-gather.5.cloned.1.call-update
  7.3 0.7 all-gather.7.cloned.1.call-update
  8.1 0.7 all-gather.9.cloned.1.call-update
  9.4 30.8 %all-gather.5.cloned.1.call-done = bf16[1024,1536]{1,0:T(8,128)(2,1)} async-done(((bf16[256,1536]{1,0:T(8,128)(2,1)}), bf16[1024,1536]{1,0:T(8,128)(2,1)}) %all-gather.5.cloned.1.call-update) | async-done | bytes 3145744 | tf_op jit(solution)/shard_map/all_gather | solution.py:45
  40.2 3.8 %convolution_bitcast_fusion = f32[2,256,1,1536]{3,1,0,2:T(8,128)S(1)} fusion(bf16[1024,1536]{1,0:T(8,128)(2,1)} %all-gather.5.cloned.1.call-done, bf16[2,1,256,1024]{3,2,1,0:T(8,128)(2,1)S(1)} %copy-done, f32[1024]{0:T(1024)S(1)} %copy-done.6, f32[2,256]{1,0:T(2,128)S(1)} %add_rsqrt_fusion.1, f32[2,256]{1,0:T(2,128)S(1)} %broadcast_multiply_fusion.1), kind=kOutput, calls=%fused_computation.6 | convolution fusion | flops 1613234176 | bytes 7348224 | tf_op jit(solution)/shard_map/dot_general | solution.py:42
  44.0 1.7 %copy-done.1 = f32[2,256,1,1536]{3,1,0,2:T(8,128)} copy-done((f32[2,256,1,1536]{3,1,0,2:T(8,128)}, f32[2,256,1,1536]{3,1,0,2:T(8,128)S(1)}, u32[]{:S(2)}) %copy-start.1) | copy-done | bytes 3145752
  45.7 1.0 copy.90
  46.7 2.8 %fusion.44 = (f32[2,256,1,512]{3,1,0,2:T(8,128)S(1)}, f32[2,256,1,512]{3,1,0,2:T(8,128)}) fusion(f32[2,256,1,1536]{3,1,0,2:T(8,128)} %copy-done.1), kind=kLoop, calls=%fused_computation.70 | loop fusion | bytes 4194304 | tf_op jit(solution)/shard_map/slice | solution.py:23
  49.5 1.6 %copy.91 = f32[2,256,1,512]{1,3,0,2:T(8,128)S(1)} copy(f32[2,256,1,512]{3,1,0,2:T(8,128)} %get-tuple-element.8) | data formatting | bytes 2097152 | tf_op jit(solution)/shard_map/slice | solution.py:22
  51.1 1.3 copy.92
  52.4 4.8 %fusion.47 = f32[2,8,256,256]{2,3,1,0:T(8,128)S(1)} fusion(f32[2,256,8,64]{1,3,2,0:T(8,128)S(1)} %bitcast.103, f32[2,256,8,64]{1,3,2,0:T(8,128)} %bitcast.104), kind=kOutput, calls=%fused_computation.73 | convolution fusion | flops 805306368 | bytes 6291456 | tf_op jit(solution)/shard_map/blmhe,bkmhe->bmhlk/dot_general | solution.py:27
  57.2 3.2 %fusion.45 = (f32[2,8,256]{2,1,0:T(8,128)S(1)}, f32[2,8,256,256]{2,3,1,0:T(8,128)S(1)}) fusion(f32[2,8,256,256]{2,3,1,0:T(8,128)S(1)} %fusion.47), kind=kOutput, calls=%fused_computation.71 | output fusion | flops 4194559 | bytes 8404992 | tf_op jit(solution)/shard_map/sub | solution.py:31
  60.9 0.5 copy.94
  61.6 2.0 %fusion.8 = bf16[512,1024]{1,0:T(8,128)(2,1)S(1)} fusion(bf16[2,1,256,1024]{3,2,1,0:T(8,128)(2,1)S(1)} %copy-done, bf16[512,512]{0,1:T(8,128)(2,1)S(1)} %bitcast.111, bf16[512,1024]{1,0:T(8,128)(2,1)} %all-gather.7.cloned.1.call-done), kind=kOutput, calls=%fused_computation.11 | convolution fusion | flops 538443776 | bytes 3670016 | tf_op jit(solution)/shard_map/dot_general | solution.py:51
  63.6 1.0 copy-done.3
  64.5 2.1 %copy.95 = bf16[2,1,256,1024]{3,0,1,2:T(2,128)(2,1)} copy(bf16[2,1,256,1024]{3,2,0,1:T(8,128)(2,1)S(1)} %bitcast.108) | data formatting | bytes 2097152 | tf_op jit(solution)/shard_map/reshape | solution.py:71
  66.6 5.5 %all-to-all-start = ((bf16[2,1,256,1024]{3,0,1,2:T(2,128)(2,1)}), bf16[2,1,256,1024]{3,0,1,2:T(2,128)(2,1)S(1)}, u32[]{:S(2)}, u32[]{:S(2)}) async-start(bf16[2,1,256,1024]{3,0,1,2:T(2,128)(2,1)} %copy.95), calls=%async_computation | async-start | bytes 2097152 | tf_op jit(solution)/shard_map/all_to_all | solution.py:72
  72.7 25.6 %all-to-all-done = bf16[2,1,256,1024]{3,0,1,2:T(2,128)(2,1)S(1)} async-done(((bf16[2,1,256,1024]{3,0,1,2:T(2,128)(2,1)}), bf16[2,1,256,1024]{3,0,1,2:T(2,128)(2,1)S(1)}, u32[]{:S(2)}, u32[]{:S(2)}) %all-to-all-start) | async-done | bytes 1048608 | tf_op jit(solution)/shard_map/all_to_all | solution.py:72
  98.3 0.7 convert.12
  99.0 0.9 convert_reduce_fusion.1
  99.9 1.8 %multiply_reduce_fusion.1 = f32[2,256]{0,1:T(8,128)S(1)} fusion(bf16[2,1,256,1024]{3,0,1,2:T(2,128)(2,1)S(1)} %all-to-all-done, f32[2,256]{0,1:T(8,128)S(1)} %broadcast_multiply_fusion), kind=kLoop, calls=%fused_computation.22 | loop fusion | flops 2096640 | bytes 1052672 | tf_op jit(solution)/shard_map/reduce_sum | solution.py:15
  102.0 4.0 %fusion.5 = f32[2,8,32,1536]{3,2,1,0:T(8,128)S(1)} fusion(bf16[1024,1536]{1,0:T(8,128)(2,1)} %all-gather.9.cloned.1.call-done, f32[2,8,32,1024]{3,0,2,1:T(2,128)S(1)} %convert.12, f32[1024]{0:T(1024)S(1)} %copy-done.7, f32[2,8,32]{2,1,0:T(8,128)S(1)} %copy.141, f32[2,8,32]{2,1,0:T(8,128)S(1)} %copy.142), kind=kOutput, calls=%fused_computation.7 | convolution fusion | flops 1612709888 | bytes 8396800 | tf_op jit(solution)/shard_map/dot_general | solution.py:42
  106.0 1.1 fusion.43
  107.2 0.9 slice.34
  108.0 1.6 %reshape.153 = f32[2,8,32,8,64]{4,3,2,1,0:T(8,128)S(1)} reshape(f32[2,8,32,512]{3,2,1,0:T(8,128)} %get-tuple-element.6) | data formatting | bytes 2097152 | tf_op jit(solution)/shard_map/reshape | solution.py:23
  109.6 1.8 %reshape.152 = f32[2,8,32,8,64]{4,3,2,1,0:T(8,128)} reshape(f32[2,8,32,512]{3,2,1,0:T(8,128)S(1)} %get-tuple-element.5) | data formatting | bytes 2097152 | tf_op jit(solution)/shard_map/reshape | solution.py:22
  111.4 7.9 %fusion.9 = f32[2,32,8,8,8]{3,4,2,1,0:T(8,128)S(1)} fusion(f32[2,8,32,8,64]{4,3,2,1,0:T(8,128)S(1)} %reshape.153, f32[2,8,32,8,64]{4,3,2,1,0:T(8,128)} %reshape.152), kind=kOutput, calls=%fused_computation.12 | convolution fusion | flops 25165824 | bytes 2228224 | tf_op jit(solution)/shard_map/blmhe,bkmhe->bmhlk/dot_general | solution.py:27
  119.3 2.3 %fusion.46 = (f32[2,32,8,8]{3,2,1,0:T(8,128)S(1)}, f32[2,32,8,8,8]{3,4,2,1,0:T(8,128)}) fusion(f32[2,32,8,8,8]{3,4,2,1,0:T(8,128)S(1)} %fusion.9), kind=kOutput, calls=%fused_computation.72 | output fusion | flops 98311 | bytes 278528 | tf_op jit(solution)/shard_map/sub | solution.py:31
  122.1 2.6 %fusion.18 = bf16[2,8,32,8,64]{4,1,3,2,0:T(8,128)(2,1)S(1)} fusion(f32[2,32,8,8,8]{3,4,2,1,0:T(8,128)} %get-tuple-element.12, bf16[2,8,32,8,64]{4,3,2,1,0:T(8,128)(2,1)S(1)} %reshape.151, f32[2,32,8,8]{3,2,1,0:T(8,128)S(1)} %get-tuple-element.11), kind=kOutput, calls=%fused_computation.31 | convolution fusion | flops 4521984 | bytes 1196032 | tf_op jit(solution)/shard_map/bmhlk,bkmhe->blmhe/dot_general | solution.py:33
  124.9 0.6 reshape.154
  125.6 18.1 %all_to_all.14 = bf16[8,2,1,32,512]{4,3,1,2,0:T(8,128)(2,1)S(1)} all-to-all(bf16[8,2,1,32,512]{4,3,1,2,0:T(8,128)(2,1)S(1)} %fusion.33), channel_id=1, replica_groups=mesh['fsdp'=4,'tm'=8] {'tm'}, dimensions={0} | all-to-all | bytes 1048576 | tf_op jit(solution)/shard_map/all_to_all | solution.py:83
  143.8 2.9 %add_convert_fusion = bf16[512,1024]{1,0:T(8,128)(2,1)} fusion(bf16[512,1024]{1,0:T(8,128)(2,1)S(1)} %copy-done.4, bf16[512,512]{1,0:T(8,128)(2,1)S(1)} %bitcast.110, bf16[512,1024]{1,0:T(8,128)(2,1)} %all-gather.11.cloned.1.call-done), kind=kOutput, calls=%fused_computation.19 | convolution fusion | flops 538443776 | bytes 3670016 | tf_op jit(solution)/shard_map/dot_general | solution.py:51
  (44 shorter events, 3.1 us)
Async XLA Ops:
  6.5 2.2 %copy-start = (bf16[2,1,256,1024]{3,2,1,0:T(8,128)(2,1)S(1)}, bf16[2,1,256,1024]{3,2,1,0:T(8,128)(2,1)}, u32[]{:S(2)}) copy-start(bf16[2,1,256,1024]{3,2,1,0:T(8,128)(2,1)} %param.7) | copy-start | bytes 3145732
  6.5 33.6 %copy-start.6 = (f32[1024]{0:T(1024)S(1)}, f32[1024]{0:T(1024)}, u32[]{:S(2)}) copy-start(f32[1024]{0:T(1024)} %param.8) | copy-start | bytes 12292
  6.5 33.6 %all-gather.5.cloned.1.call-start = ((), (), s32[]{:S(2)}) async-start(), calls=%async_computation.2 | async-start | bytes 3932160 | tf_op jit(solution)/shard_map/all_gather | solution.py:45
  7.3 54.3 %all-gather.7.cloned.1.call-start = ((), (), s32[]{:S(2)}) async-start(), calls=%async_computation.3 | async-start | bytes 1310720 | tf_op jit(solution)/shard_map/all_gather | solution.py:54
  8.0 94.0 %all-gather.9.cloned.1.call-start = ((), (), s32[]{:S(2)}) async-start(), calls=%async_computation.4 | async-start | bytes 3932160 | tf_op jit(solution)/shard_map/all_gather | solution.py:45
  44.0 1.7 %copy-start.1 = (f32[2,256,1,1536]{3,1,0,2:T(8,128)}, f32[2,256,1,1536]{3,1,0,2:T(8,128)S(1)}, u32[]{:S(2)}) copy-start(f32[2,256,1,1536]{3,1,0,2:T(8,128)S(1)} %convolution_bitcast_fusion) | copy-start | bytes 9437188
  57.2 3.3 %copy-start.5 = (bf16[2,256,1,512]{1,3,0,2:T(8,128)(2,1)S(1)}, bf16[2,256,1,512]{1,3,0,2:T(8,128)(2,1)}, u32[]{:S(2)}) copy-start(bf16[2,256,1,512]{1,3,0,2:T(8,128)(2,1)} %copy.90) | copy-start | bytes 1572868
  63.6 1.0 copy-start.3
  66.6 31.7 %all-to-all-start = ((bf16[2,1,256,1024]{3,0,1,2:T(2,128)(2,1)}), bf16[2,1,256,1024]{3,0,1,2:T(2,128)(2,1)S(1)}, u32[]{:S(2)}, u32[]{:S(2)}) async-start(bf16[2,1,256,1024]{3,0,1,2:T(2,128)(2,1)} %copy.95), calls=%async_computation | async-start | bytes 2097152 | tf_op jit(solution)/shard_map/all_to_all | solution.py:72
  72.1 71.7 %all-gather.11.cloned.1.call-start = ((), (), s32[]{:S(2)}) async-start(), calls=%async_computation.5 | async-start | bytes 1310720 | tf_op jit(solution)/shard_map/all_gather | solution.py:54
  99.0 3.0 %copy-start.7 = (f32[1024]{0:T(1024)S(1)}, f32[1024]{0:T(1024)}, u32[]{:S(2)}) copy-start(f32[1024]{0:T(1024)} %param.11) | copy-start | bytes 12292
  119.3 2.3 %copy-start.2 = (bf16[2,8,32,512]{3,2,1,0:T(8,128)(2,1)S(1)}, bf16[2,8,32,512]{3,2,1,0:T(8,128)(2,1)}, u32[]{:S(2)}) copy-start(bf16[2,8,32,512]{3,2,1,0:T(8,128)(2,1)} %slice.34) | copy-start | bytes 1572868
  124.9 18.9 %copy-start.4 = (bf16[512,1024]{1,0:T(8,128)(2,1)S(1)}, bf16[512,1024]{1,0:T(8,128)(2,1)}, u32[]{:S(2)}) copy-start(bf16[512,1024]{1,0:T(8,128)(2,1)} %copy-done.3) | copy-start | bytes 3145732
Sparse Core Ops, SparseCore 0:
  8.9 31.2 all-gather.4
  41.7 16.6 all-gather.6
  60.0 28.4 all-gather.8
  90.0 16.6 all-gather.10
